TPU v7x, 512 devices: a whole 4x8x8 slice. The times are simulated.
512 devices in a mesh: row: 16 (over y, core), col: 32 (over z, x).
Axes of the slice: x: 4, y: 8, z: 8, core: 2. Of those that a mesh axis runs over, the one named last changes fastest.
Arguments:
- templates: float32 [1536, 3, 1024], P(('row', 'col')), may hold values from -600 to 600
Outputs:
- similar: float32 [1536, 1536], P(('row', 'col'))
All inputs are finite; a program needn't handle non-finite values.
Results may differ from a plain program's by a relative error of at most 0.0012.
Values may be sent and summed in bfloat16 or wider, within the bound.
No kernel may reach another device: no remote copies, remote signals or barrier semaphores. Data moves between devices by JAX's collectives and lax.ppermute only.
A program may use at most 128 MiB of HBM per device.

v0:
```python
import math
import jax
import jax.numpy as jnp
from jax import lax
from jax.sharding import PartitionSpec as P

LAGS = 512


def copy_for_each(array, axis):
    copies = jnp.broadcast_to(array, (lax.axis_size(axis), *array.shape))
    return lax.all_to_all(copies, axis, split_axis=0, concat_axis=0, tiled=True)


def in_order(tiles, dim):
    shape = list(tiles.shape[1:])
    shape[dim] *= tiles.shape[0]
    return jnp.moveaxis(tiles, 0, dim).reshape(shape)


def collect(array, axis, dim):
    tiles = copy_for_each(array, axis)
    return in_order(tiles, dim)


def normalize(templates):
    scaling = lax.rsqrt(jnp.mean(templates * templates, axis=2, keepdims=True) + 1e-06) / math.sqrt(
        templates.shape[2]
    )
    return (templates * scaling).astype(jnp.bfloat16)


def forward_table(samples, transform_len):
    half_len = transform_len // 2
    sample_idx = jnp.arange(samples, dtype=jnp.int32)[:, None]
    slot_idx = jnp.arange(transform_len, dtype=jnp.int32)[None, :]
    freq_idx = jnp.where(slot_idx < half_len, slot_idx, slot_idx - half_len)
    phases = sample_idx * freq_idx % transform_len
    angles = phases.astype(jnp.float32) * (2.0 * math.pi / transform_len)
    nyquist = jnp.where(sample_idx % 2 == 0, 1.0, -1.0)
    basis = jnp.where(
        slot_idx < half_len,
        jnp.cos(angles),
        jnp.where(slot_idx == half_len, nyquist, -jnp.sin(angles)),
    )
    return basis.astype(jnp.bfloat16)


def inverse_table(transform_len, lag_total):
    half_len = transform_len // 2
    slot_idx = jnp.arange(transform_len, dtype=jnp.int32)[:, None]
    lag_idx = jnp.arange(lag_total, dtype=jnp.int32)[None, :] - lag_total // 2
    freq_idx = jnp.where(slot_idx < half_len, slot_idx, slot_idx - half_len)
    phases = freq_idx * lag_idx % transform_len
    angles = phases.astype(jnp.float32) * (2.0 * math.pi / transform_len)
    weight = jnp.where(freq_idx == 0, 1.0, 2.0) / transform_len
    nyquist = jnp.where(lag_idx % 2 == 0, 1.0, -1.0) / transform_len
    basis = jnp.where(
        slot_idx < half_len,
        weight * jnp.cos(angles),
        jnp.where(slot_idx == half_len, nyquist, -weight * jnp.sin(angles)),
    )
    return basis.astype(jnp.bfloat16)


def spectra_of(normed, basis):
    row_total, comps, samples = normed.shape
    flattened = normed.reshape(row_total * comps, samples)
    spectrum = jnp.dot(flattened, basis, preferred_element_type=jnp.float32)
    return spectrum.astype(jnp.bfloat16).reshape(row_total, comps, basis.shape[1])


def pair_einsum(left_part, right_part):
    return jnp.einsum("icf,jcf->ijf", left_part.astype(jnp.float32), right_part.astype(jnp.float32))


def similarity(left_spec, right_spec, inverse):
    half_len = left_spec.shape[2] // 2
    left_real = left_spec[:, :, :half_len]
    left_imag = left_spec[:, :, half_len:]
    right_real = right_spec[:, :, :half_len]
    right_imag = right_spec[:, :, half_len:]
    above_zero = jnp.arange(half_len, dtype=jnp.int32) >= 1
    right_masked = jnp.where(above_zero, right_imag, jnp.zeros_like(right_imag))
    left_masked = jnp.where(above_zero, left_real, jnp.zeros_like(left_real))
    right_turned = jnp.where(above_zero, -right_real, right_imag)
    even_part = pair_einsum(
        jnp.concatenate([left_real, left_imag], axis=1),
        jnp.concatenate([right_real, right_masked], axis=1),
    )
    odd_part = pair_einsum(
        jnp.concatenate([left_masked, left_imag], axis=1),
        jnp.concatenate([right_imag, right_turned], axis=1),
    )
    cross_spec = jnp.concatenate([even_part, odd_part], axis=2).astype(jnp.bfloat16)
    left_rows = left_spec.shape[0]
    right_rows = right_spec.shape[0]
    lagged = jnp.dot(
        cross_spec.reshape(left_rows * right_rows, 2 * half_len),
        inverse,
        preferred_element_type=jnp.float32,
    )
    return jnp.max(lagged, axis=1).reshape(left_rows, right_rows)


def body(templates):
    per_device = templates.shape[0]
    samples = templates.shape[2]
    transform_len = samples + LAGS // 2
    forward = forward_table(samples, transform_len)
    inverse = inverse_table(transform_len, LAGS)
    local_waves = normalize(templates)
    outgoing = spectra_of(local_waves, forward)
    row_count = lax.axis_size("row")
    col_count = lax.axis_size("col")
    partners = collect(outgoing, "row", 0)
    pair_block = similarity(collect(outgoing, "col", 0), partners, inverse)
    owned_rows = lax.all_to_all(pair_block, "col", split_axis=0, concat_axis=1, tiled=True)
    reordered = owned_rows.reshape(per_device, col_count, row_count, per_device).transpose(
        0, 2, 1, 3
    )
    return reordered.reshape(per_device, col_count * row_count * per_device)


def solution(mesh):
    placed = (P(("row", "col"), None, None),)
    return jax.shard_map(
        body, mesh=mesh, in_specs=placed, out_specs=P(("row", "col"), None), check_vma=False
    )
```

profile of v0, /device:TPU:1, one launch (start us, length us, event | category | flops | bytes accessed | tf_op | source)
XLA Modules:
  0.0 158.0 jit_solution(2501880423134903222)
XLA Ops:
  0.0 0.9 multiply_reduce_fusion
  0.9 0.9 multiply_convert_fusion
  1.8 22.6 %fusion.20 = bf16[9,1280]{1,0:T(8,128)(2,1)S(1)} fusion(bf16[9,1024]{1,0:T(8,128)(2,1)S(1)} %reshape.135, bf16[1024]{0:T(1024)(128)(2,1)S(1)} %fusion.37, s32[1280]{0:T(1024)S(1)} %add_select_fusion.2, pred[1280]{0:T(1024)(128)(4,1)S(1)} %get-tuple-element.11, pred[1280]{0:T(1024)(128)(4,1)S(1)} %get-tuple-element.12), kind=kOutput, calls=%fused_computation.26 | convolution fusion | flops 39333120 | bytes 51200 | tf_op jit(solution)/shard_map/dot_general | solution.py:69
  24.5 0.1 broadcast_in_dim.105
  24.6 25.9 %all_to_all.26 = bf16[16,3,3,1280]{3,1,2,0:T(4,128)(2,1)S(1)} all-to-all(bf16[16,3,3,1280]{3,1,2,0:T(4,128)(2,1)S(1)} %broadcast_in_dim.105), channel_id=1, replica_groups=mesh['row'=16,'col'=32] {'row'}, dimensions={0} | all-to-all | bytes 737280 | tf_op jit(solution)/shard_map/all_to_all | solution.py:12
  50.5 1.2 broadcast_in_dim.108
  51.7 12.1 %all-to-all-start.1 = ((bf16[32,3,3,1280]{3,1,2,0:T(4,128)(2,1)}), bf16[32,3,3,1280]{3,1,2,0:T(4,128)(2,1)S(1)}, u32[]{:S(2)}, u32[]{:S(2)}) async-start(bf16[32,3,3,1280]{3,1,2,0:T(4,128)(2,1)} %broadcast_in_dim.108), calls=%async_computation.1 | async-start | bytes 1966080 | tf_op jit(solution)/shard_map/all_to_all | solution.py:12
  63.9 13.3 %select_convert_fusion.11 = bf16[1280,512]{1,0:T(8,128)(2,1)} fusion(f32[1280]{0:T(1024)S(1)} %get-tuple-element.14, bf16[512]{0:T(512)(128)(2,1)S(1)} %select_multiply_fusion.1, s32[512]{0:T(512)S(1)} %iota_add_fusion, s32[1280]{0:T(1024)S(1)} %add_select_fusion.2, f32[1280]{0:T(1024)S(1)} %get-tuple-element.13, ...), kind=kLoop, calls=%fused_computation.17.clone.clone.2 | loop fusion | flops 8519680 | bytes 1331712 | tf_op jit(solution)/shard_map/dot_general | solution.py:98
  77.2 0.2 copy.15
  77.4 0.3 reshape.137
  77.8 1.3 copy.22
  79.2 1.8 %copy.20 = bf16[48,6,640]{0,1,2:T(8,128)(2,1)} copy(bf16[48,6,640]{2,0,1:T(8,128)(2,1)S(1)} %pad_maximum_fusion.4) | data formatting | bytes 737280 | tf_op jit(solution)/shard_map/concatenate | solution.py:89
  81.0 9.1 %all-to-all-done.1 = bf16[32,3,3,1280]{3,1,2,0:T(4,128)(2,1)S(1)} async-done(((bf16[32,3,3,1280]{3,1,2,0:T(4,128)(2,1)}), bf16[32,3,3,1280]{3,1,2,0:T(4,128)(2,1)S(1)}, u32[]{:S(2)}, u32[]{:S(2)}) %all-to-all-start.1) | async-done | bytes 737312 | tf_op jit(solution)/shard_map/all_to_all | solution.py:12
  90.1 1.3 copy.17
  91.4 2.3 %reshape.138 = bf16[96,3,1280]{2,0,1:T(8,128)(2,1)S(1)} reshape(bf16[32,3,3,1280]{3,1,0,2:T(4,128)(2,1)} %copy.17) | data formatting | bytes 1474560 | tf_op jit(solution)/shard_map/reshape | solution.py:18
  93.7 0.8 fusion.50
  94.6 0.8 copy.26
  95.4 2.4 %broadcast_select_fusion = bf16[96,3,640]{0,1,2:T(4,128)(2,1)S(1)} fusion(bf16[96,3,640]{0,1,2:T(4,128)(2,1)S(1)} %copy.26, pred[640]{0:T(1024)(128)(4,1)S(1)} %iota_compare_fusion.2), kind=kLoop, calls=%fused_computation.41 | loop fusion | flops 184320 | bytes 737920 | tf_op jit(solution)/shard_map/jit(_where)/select_n | solution.py:85
  97.8 1.7 %copy.27 = bf16[96,3,640]{0,1,2:T(4,128)(2,1)S(1)} copy(bf16[96,3,640]{2,0,1:T(8,128)(2,1)} %get-tuple-element.6) | data formatting | bytes 737280
  99.4 4.5 %convert_bitcast_fusion = bf16[96,48,640]{0,1,2:T(8,128)(2,1)} fusion(bf16[48,6,640]{0,1,2:T(8,128)(2,1)S(1)} %copy.22, bf16[96,3,640]{0,1,2:T(4,128)(2,1)S(1)} %copy.27, bf16[96,3,640]{0,1,2:T(4,128)(2,1)S(1)} %broadcast_select_fusion), kind=kOutput, calls=%fused_computation.4 | convolution fusion | flops 39813120 | bytes 7004160 | tf_op jit(solution)/shard_map/icf,jcf->ijf/dot_general | solution.py:74
  103.9 11.5 %copy.23 = bf16[96,48,640]{2,1,0:T(8,128)(2,1)} copy(bf16[96,48,640]{0,1,2:T(8,128)(2,1)} %convert_bitcast_fusion) | data formatting | bytes 11796480 | tf_op jit(solution)/shard_map/icf,jcf->ijf/transpose | solution.py:74
  115.4 4.5 %convert_bitcast_fusion.1 = bf16[96,48,640]{0,1,2:T(8,128)(2,1)} fusion(bf16[48,6,640]{0,1,2:T(8,128)(2,1)S(1)} %copy-done, bf16[96,3,640]{0,1,2:T(4,128)(2,1)S(1)} %copy.27, bf16[96,3,640]{0,1,2:T(4,128)(2,1)S(1)} %copy.26), kind=kOutput, calls=%fused_computation.5 | convolution fusion | flops 39813120 | bytes 7004160 | tf_op jit(solution)/shard_map/icf,jcf->ijf/dot_general | solution.py:74
  119.8 11.4 %copy.21 = bf16[96,48,640]{2,1,0:T(8,128)(2,1)} copy(bf16[96,48,640]{0,1,2:T(8,128)(2,1)} %convert_bitcast_fusion.1) | data formatting | bytes 11796480 | tf_op jit(solution)/shard_map/icf,jcf->ijf/transpose | solution.py:74
  131.2 9.6 %fusion.17 = f32[4608]{0:T(1024)S(1)} fusion(bf16[4608,640]{1,0:T(8,128)(2,1)} %bitcast.21, bf16[4608,640]{1,0:T(8,128)(2,1)} %bitcast.22, bf16[1280,512]{1,0:T(8,128)(2,1)S(1)} %copy-done.1), kind=kOutput, calls=%fused_computation.25 | convolution fusion | flops 6065745408 | bytes 13125632 | tf_op jit(solution)/shard_map/dot_general | solution.py:98
  140.9 0.1 all_to_all.20
  141.0 0.1 reshape.141
  141.1 14.0 %all_to_all.27 = f32[32,1,144]{2,1,0:T(1,128)S(1)} all-to-all(f32[32,1,144]{2,1,0:T(1,128)S(1)} %reshape.141), channel_id=1, replica_groups=mesh['row'=16,'col'=32] {'col'}, dimensions={0} | all-to-all | bytes 36864 | tf_op jit(solution)/shard_map/all_to_all | solution.py:118
  155.1 0.5 broadcast.247
  155.6 0.7 reduce
  156.3 0.1 reshape.142
  156.6 0.4 copy.25
  156.9 1.1 reshape.140
  (20 shorter events, 0.4 us)
Async XLA Ops:
  51.7 38.4 %all-to-all-start.1 = ((bf16[32,3,3,1280]{3,1,2,0:T(4,128)(2,1)}), bf16[32,3,3,1280]{3,1,2,0:T(4,128)(2,1)S(1)}, u32[]{:S(2)}, u32[]{:S(2)}) async-start(bf16[32,3,3,1280]{3,1,2,0:T(4,128)(2,1)} %broadcast_in_dim.108), calls=%async_computation.1 | async-start | bytes 1966080 | tf_op jit(solution)/shard_map/all_to_all | solution.py:12
  103.9 11.5 %copy-start = (bf16[48,6,640]{0,1,2:T(8,128)(2,1)S(1)}, bf16[48,6,640]{0,1,2:T(8,128)(2,1)}, u32[]{:S(2)}) copy-start(bf16[48,6,640]{0,1,2:T(8,128)(2,1)} %copy.20) | copy-start | bytes 1105924
  119.8 11.4 %copy-start.1 = (bf16[1280,512]{1,0:T(8,128)(2,1)S(1)}, bf16[1280,512]{1,0:T(8,128)(2,1)}, u32[]{:S(2)}) copy-start(bf16[1280,512]{1,0:T(8,128)(2,1)} %select_convert_fusion.11) | copy-start | bytes 3932164
where the time goes:
time: 159 us; the launch traced here: 158 us
  matrix products  41.2 us (26%)
  blocking collectives  39.9 us (25%)
  local copies, waits for them, and re-layouts  37.2 us (23%)
  other arithmetic  18.4 us (12%)
  starting transfers between devices  12.1 us (8%)
  waiting for transfers between devices  9.09 us (6%)
    all_to_all x1, blocking collectives, copy_for_each(): return lax.all_to_all(copies, axis, split_axis=0, concat_axis=0, tiled=True)  25.9 us
    transpose x2, local copies, waits for them, and re-layouts, pair_einsum(): jnp.einsum('icf,jcf->ijf', left_part.astype(jnp.float32), right_part.asty...  22.9 us
    dot_general x1, matrix products, spectra_of(): spectrum = jnp.dot(flattened, basis, preferred_element_type=jnp.float32)  22.6 us
    all_to_all x1, blocking collectives, body(): lax.all_to_all(pair_block, 'col', split_axis=0, concat_axis=1, tiled=True)  14 us
    dot_general x1, other arithmetic, similarity(): jnp.dot(cross_spec.reshape(left_rows * right_rows, 2 * half_len), inverse...  13.3 us
    all_to_all x1, starting transfers between devices, copy_for_each(): return lax.all_to_all(copies, axis, split_axis=0, concat_axis=0, tiled=True)  12.1 us
    dot_general x1, matrix products, similarity(): jnp.dot(cross_spec.reshape(left_rows * right_rows, 2 * half_len), inverse...  9.65 us
    all_to_all x1, waiting for transfers between devices, copy_for_each(): return lax.all_to_all(copies, axis, split_axis=0, concat_axis=0, tiled=True)  9.09 us
  transfers between devices with their start and end apart: 1, of which 1 were waited for; matrix products, arithmetic and copies ran while one was open for 11% of the time, Pallas kernels for 0%

commit v1 on v0

--- a/solution.py
+++ b/solution.py
@@ -115,7 +115,10 @@
     col_count = lax.axis_size("col")
     partners = collect(outgoing, "row", 0)
     pair_block = similarity(collect(outgoing, "col", 0), partners, inverse)
-    owned_rows = lax.all_to_all(pair_block, "col", split_axis=0, concat_axis=1, tiled=True)
+    owned_rows = jnp.concatenate(
+        lax.all_to_all(jnp.stack(jnp.split(pair_block, lax.axis_size("col"), axis=0)), "col", 0, 0),
+        axis=1,
+    )
     reordered = owned_rows.reshape(per_device, col_count, row_count, per_device).transpose(
         0, 2, 1, 3
     )

time: 159 us -> 162 us (1.019)
  local copies, waits for them, and re-layouts: 37.2 us -> 40.3 us
    another operation x0 -> x34, local copies, waits for them, and re-layouts: none -> 2.67 us  [the longest x33 2.64 us: body(): jnp.stack(jnp.split(pair_block, lax.axis_size('col'), axis=0))]
where the time goes in v1:
time: 162 us; the launch traced here: 161 us
  matrix products  41.1 us (25%)
  local copies, waits for them, and re-layouts  40.3 us (25%)
  blocking collectives  39.9 us (25%)
  other arithmetic  18.4 us (11%)
  starting transfers between devices  12.1 us (7%)
  waiting for transfers between devices  9.11 us (6%)
    all_to_all x1, blocking collectives, copy_for_each(): return lax.all_to_all(copies, axis, split_axis=0, concat_axis=0, tiled=True)  25.9 us
    transpose x2, local copies, waits for them, and re-layouts, pair_einsum(): jnp.einsum('icf,jcf->ijf', left_part.astype(jnp.float32), right_part.asty...  22.9 us
    dot_general x1, matrix products, spectra_of(): spectrum = jnp.dot(flattened, basis, preferred_element_type=jnp.float32)  22.6 us
    all_to_all x1, blocking collectives, body(): lax.all_to_all(jnp.stack(jnp.split(pair_block, lax.axis_size('col'), axis...  14 us
    dot_general x1, other arithmetic, similarity(): jnp.dot(cross_spec.reshape(left_rows * right_rows, 2 * half_len), inverse...  13.3 us
    all_to_all x1, starting transfers between devices, copy_for_each(): return lax.all_to_all(copies, axis, split_axis=0, concat_axis=0, tiled=True)  12.1 us
    dot_general x1, matrix products, similarity(): jnp.dot(cross_spec.reshape(left_rows * right_rows, 2 * half_len), inverse...  9.53 us
    all_to_all x1, waiting for transfers between devices, copy_for_each(): return lax.all_to_all(copies, axis, split_axis=0, concat_axis=0, tiled=True)  9.11 us
  transfers between devices with their start and end apart: 1, of which 1 were waited for; matrix products, arithmetic and copies ran while one was open for 11% of the time, Pallas kernels for 0%

profile of v1, /device:TPU:1, one launch (start us, length us, event | category | flops | bytes accessed | tf_op | source)
XLA Modules:
  0.0 161.1 jit_solution(16871548208129322738)
XLA Ops:
  0.0 0.9 multiply_reduce_fusion
  0.9 0.9 multiply_convert_fusion
  1.8 22.6 %fusion.20 = bf16[9,1280]{1,0:T(8,128)(2,1)S(1)} fusion(bf16[9,1024]{1,0:T(8,128)(2,1)S(1)} %reshape.450, bf16[1024]{0:T(1024)(128)(2,1)S(1)} %fusion.37, s32[1280]{0:T(1024)S(1)} %add_select_fusion.2, pred[1280]{0:T(1024)(128)(4,1)S(1)} %get-tuple-element.43, pred[1280]{0:T(1024)(128)(4,1)S(1)} %get-tuple-element.44), kind=kOutput, calls=%fused_computation.26 | convolution fusion | flops 39333120 | bytes 51200 | tf_op jit(solution)/shard_map/dot_general | solution.py:69
  24.5 0.1 broadcast_in_dim.105
  24.6 25.9 %all_to_all.15 = bf16[16,3,3,1280]{3,1,2,0:T(4,128)(2,1)S(1)} all-to-all(bf16[16,3,3,1280]{3,1,2,0:T(4,128)(2,1)S(1)} %broadcast_in_dim.105), channel_id=1, replica_groups=mesh['row'=16,'col'=32] {'row'}, dimensions={0} | all-to-all | bytes 737280 | tf_op jit(solution)/shard_map/all_to_all | solution.py:12
  50.5 1.2 broadcast_in_dim.108
  51.8 12.1 %all-to-all-start.1 = ((bf16[32,3,3,1280]{3,1,2,0:T(4,128)(2,1)}), bf16[32,3,3,1280]{3,1,2,0:T(4,128)(2,1)S(1)}, u32[]{:S(2)}, u32[]{:S(2)}) async-start(bf16[32,3,3,1280]{3,1,2,0:T(4,128)(2,1)} %broadcast_in_dim.108), calls=%async_computation.1 | async-start | bytes 1966080 | tf_op jit(solution)/shard_map/all_to_all | solution.py:12
  63.9 13.3 %select_convert_fusion.11 = bf16[1280,512]{1,0:T(8,128)(2,1)} fusion(f32[1280]{0:T(1024)S(1)} %get-tuple-element.46, bf16[512]{0:T(512)(128)(2,1)S(1)} %select_multiply_fusion.1, s32[512]{0:T(512)S(1)} %iota_add_fusion, s32[1280]{0:T(1024)S(1)} %add_select_fusion.2, f32[1280]{0:T(1024)S(1)} %get-tuple-element.45, ...), kind=kLoop, calls=%fused_computation.17.clone.clone.2 | loop fusion | flops 8519680 | bytes 1331712 | tf_op jit(solution)/shard_map/dot_general | solution.py:98
  77.2 0.2 copy.15
  77.4 0.3 reshape.452
  77.8 1.3 copy.22
  79.2 1.8 %copy.20 = bf16[48,6,640]{0,1,2:T(8,128)(2,1)} copy(bf16[48,6,640]{2,0,1:T(8,128)(2,1)S(1)} %pad_maximum_fusion.4) | data formatting | bytes 737280 | tf_op jit(solution)/shard_map/concatenate | solution.py:89
  81.0 9.1 %all-to-all-done.1 = bf16[32,3,3,1280]{3,1,2,0:T(4,128)(2,1)S(1)} async-done(((bf16[32,3,3,1280]{3,1,2,0:T(4,128)(2,1)}), bf16[32,3,3,1280]{3,1,2,0:T(4,128)(2,1)S(1)}, u32[]{:S(2)}, u32[]{:S(2)}) %all-to-all-start.1) | async-done | bytes 737312 | tf_op jit(solution)/shard_map/all_to_all | solution.py:12
  90.1 1.3 copy.17
  91.4 2.3 %reshape.453 = bf16[96,3,1280]{2,0,1:T(8,128)(2,1)S(1)} reshape(bf16[32,3,3,1280]{3,1,0,2:T(4,128)(2,1)} %copy.17) | data formatting | bytes 1474560 | tf_op jit(solution)/shard_map/reshape | solution.py:18
  93.7 0.8 fusion.50
  94.6 0.8 copy.26
  95.4 2.4 %broadcast_select_fusion = bf16[96,3,640]{0,1,2:T(4,128)(2,1)S(1)} fusion(bf16[96,3,640]{0,1,2:T(4,128)(2,1)S(1)} %copy.26, pred[640]{0:T(1024)(128)(4,1)S(1)} %iota_compare_fusion.2), kind=kLoop, calls=%fused_computation.41 | loop fusion | flops 184320 | bytes 737920 | tf_op jit(solution)/shard_map/jit(_where)/select_n | solution.py:85
  97.8 1.7 %copy.27 = bf16[96,3,640]{0,1,2:T(4,128)(2,1)S(1)} copy(bf16[96,3,640]{2,0,1:T(8,128)(2,1)} %get-tuple-element.6) | data formatting | bytes 737280
  99.4 4.5 %convert_bitcast_fusion = bf16[96,48,640]{0,1,2:T(8,128)(2,1)} fusion(bf16[48,6,640]{0,1,2:T(8,128)(2,1)S(1)} %copy.22, bf16[96,3,640]{0,1,2:T(4,128)(2,1)S(1)} %copy.27, bf16[96,3,640]{0,1,2:T(4,128)(2,1)S(1)} %broadcast_select_fusion), kind=kOutput, calls=%fused_computation.4 | convolution fusion | flops 39813120 | bytes 7004160 | tf_op jit(solution)/shard_map/icf,jcf->ijf/dot_general | solution.py:74
  103.9 11.4 %copy.23 = bf16[96,48,640]{2,1,0:T(8,128)(2,1)} copy(bf16[96,48,640]{0,1,2:T(8,128)(2,1)} %convert_bitcast_fusion) | data formatting | bytes 11796480 | tf_op jit(solution)/shard_map/icf,jcf->ijf/transpose | solution.py:74
  115.4 4.5 %convert_bitcast_fusion.1 = bf16[96,48,640]{0,1,2:T(8,128)(2,1)} fusion(bf16[48,6,640]{0,1,2:T(8,128)(2,1)S(1)} %copy-done, bf16[96,3,640]{0,1,2:T(4,128)(2,1)S(1)} %copy.27, bf16[96,3,640]{0,1,2:T(4,128)(2,1)S(1)} %copy.26), kind=kOutput, calls=%fused_computation.5 | convolution fusion | flops 39813120 | bytes 7004160 | tf_op jit(solution)/shard_map/icf,jcf->ijf/dot_general | solution.py:74
  119.8 11.5 %copy.21 = bf16[96,48,640]{2,1,0:T(8,128)(2,1)} copy(bf16[96,48,640]{0,1,2:T(8,128)(2,1)} %convert_bitcast_fusion.1) | data formatting | bytes 11796480 | tf_op jit(solution)/shard_map/icf,jcf->ijf/transpose | solution.py:74
  131.3 9.5 %fusion.17 = f32[4608]{0:T(1024)S(1)} fusion(bf16[4608,640]{1,0:T(8,128)(2,1)} %bitcast.21, bf16[4608,640]{1,0:T(8,128)(2,1)} %bitcast.22, bf16[1280,512]{1,0:T(8,128)(2,1)S(1)} %copy-done.1), kind=kOutput, calls=%fused_computation.25 | convolution fusion | flops 6065745408 | bytes 13125632 | tf_op jit(solution)/shard_map/dot_general | solution.py:98
  144.1 0.1 reshape.456
  144.2 14.0 %all_to_all.16 = f32[32,1,144]{2,1,0:T(1,128)S(1)} all-to-all(f32[32,1,144]{2,1,0:T(1,128)S(1)} %reshape.456), channel_id=1, replica_groups=mesh['row'=16,'col'=32] {'col'}, dimensions={0} | all-to-all | bytes 36864 | tf_op jit(solution)/shard_map/all_to_all | solution.py:119
  158.2 0.5 broadcast.247
  158.7 0.7 reduce
  159.4 0.1 reshape.457
  159.5 0.1 copy.24
  159.7 0.4 copy.25
  160.0 1.1 reshape.455
  (85 shorter events, 3.4 us)
Async XLA Ops:
  51.8 38.4 %all-to-all-start.1 = ((bf16[32,3,3,1280]{3,1,2,0:T(4,128)(2,1)}), bf16[32,3,3,1280]{3,1,2,0:T(4,128)(2,1)S(1)}, u32[]{:S(2)}, u32[]{:S(2)}) async-start(bf16[32,3,3,1280]{3,1,2,0:T(4,128)(2,1)} %broadcast_in_dim.108), calls=%async_computation.1 | async-start | bytes 1966080 | tf_op jit(solution)/shard_map/all_to_all | solution.py:12
  103.9 11.4 %copy-start = (bf16[48,6,640]{0,1,2:T(8,128)(2,1)S(1)}, bf16[48,6,640]{0,1,2:T(8,128)(2,1)}, u32[]{:S(2)}) copy-start(bf16[48,6,640]{0,1,2:T(8,128)(2,1)} %copy.20) | copy-start | bytes 1105924
  119.8 11.5 %copy-start.1 = (bf16[1280,512]{1,0:T(8,128)(2,1)S(1)}, bf16[1280,512]{1,0:T(8,128)(2,1)}, u32[]{:S(2)}) copy-start(bf16[1280,512]{1,0:T(8,128)(2,1)} %select_convert_fusion.11) | copy-start | bytes 3932164
